TPU v7x, 512 devices: a whole 4x8x8 slice. The times are simulated.
512 devices in a mesh: row: 64 (over y, z), col: 8 (over x, core).
Axes of the slice: x: 4, y: 8, z: 8, core: 2. Of those that a mesh axis runs over, the one named last changes fastest.
Arguments:
- new_aux: bfloat16 [8192, 4096], P('row', 'col'), may hold values from -6 to 6
- former_auxiliary_rows: bfloat16 [81920, 4096], P('row', 'col'), may hold values from -6 to 6
- old_emb: bfloat16 [81920, 4096], P('row', 'col'), may hold values from -6 to 6
- neighbour_ids: int32 [8192, 16], P('row'), may hold values from -1 to 81919, as said below
- neighbour_counts: int32 [8192], P('row'), may hold values from 8 to 16
Outputs:
- new_emb: bfloat16 [8192, 4096], P('row', 'col')
Inputs may be any that keep to these rules, and one draw needn't show every extreme that they name: neighbour_ids[j, k] is an old row number for k < neighbour_counts[j] and -1 otherwise. The live entries of the 128 new rows of one index of row name at most 48 entries, and at most 24 different rows, within one block of 1280 old rows held by one index of row; both bounds are reached in every draw.
All inputs are finite; a program needn't handle non-finite values.
Results may differ from a plain program's by a relative error of at most 0.0049.
Values may be sent and summed in bfloat16 or wider, within the bound.
A program may use at most 64 MiB of HBM per device.

v0:
```python
import jax
import jax.numpy as jnp
from jax import lax
from jax.sharding import PartitionSpec as P

eps = 1e-06
exponential_sharpness = 0.025


def sent_to_all(x, axis):
    length = lax.axis_size(axis)
    return lax.all_to_all(jnp.broadcast_to(x[None], (length, *x.shape)), axis, 0, 0, tiled=True)


def over_copies(x, axis):
    everything = sent_to_all(x, axis)
    return jnp.sum(everything, axis=0)


def packed_total(arrays, axis):
    ends = [0]
    for a in arrays:
        ends.append(ends[-1] + a.size)
    total = over_copies(jnp.concatenate([a.ravel() for a in arrays]), axis)
    return tuple((total[b:e].reshape(a.shape) for a, b, e in zip(arrays, ends, ends[1:])))


def local(new_aux, former_auxiliary_rows, old_emb, neighbour_ids, neighbour_counts):
    devices = lax.axis_size("row")
    old_dev = former_auxiliary_rows.shape[0]
    new_dev, slots_row = neighbour_ids.shape
    width = new_aux.shape[1]
    capacity = 24 * new_dev // devices
    admissible_flags = jnp.arange(slots_row, dtype=jnp.int32)[None, :] < neighbour_counts[:, None]
    flat_ids = neighbour_ids.reshape(-1)
    flat_live = admissible_flags.reshape(-1)
    owners = jnp.where(flat_live, flat_ids // old_dev, devices)
    local_rows = jnp.where(flat_live, flat_ids - owners * old_dev, 0)
    onehot = (owners[:, None] == jnp.arange(devices, dtype=jnp.int32)[None, :]).astype(jnp.int32)
    ranks = jnp.sum(onehot * (jnp.cumsum(onehot, axis=0) - 1), axis=1)
    slots = jnp.where(flat_live, owners * capacity + ranks, devices * capacity)
    requests = jnp.full((devices * capacity + 1,), -1, jnp.int32).at[slots].set(local_rows)
    requests = requests[:-1].reshape(devices, capacity)
    clipped_owner = jnp.clip(owners, 0, devices - 1)
    distinct = capacity // 2
    sorted_sequence = jnp.sort(requests, axis=1)
    previous = jnp.concatenate(
        [jnp.full((devices, 1), -1, jnp.int32), sorted_sequence[:, :-1]], axis=1
    )
    first = (sorted_sequence >= 0) & (sorted_sequence != previous)
    position = jnp.cumsum(first.astype(jnp.int32), axis=1) - 1
    target = jnp.where(first, position, distinct)
    compact = jnp.full((devices, distinct + 1), -1, jnp.int32)
    compact = compact.at[jnp.arange(devices, dtype=jnp.int32)[:, None], target].set(
        sorted_sequence
    )[:, :distinct]
    candidates = compact[clipped_owner]
    matches = (candidates == local_rows[:, None]).astype(jnp.int32)
    found = jnp.sum(matches * jnp.arange(distinct, dtype=jnp.int32)[None, :], axis=1)
    entry_slot = clipped_owner * distinct + found
    safe = jnp.clip(
        lax.all_to_all(compact, "row", split_axis=0, concat_axis=0, tiled=True), 0, old_dev - 1
    )
    aux_rows = jnp.take(former_auxiliary_rows, safe, axis=0)
    emb_rows = jnp.take(old_emb, safe, axis=0)
    aux_back = lax.all_to_all(aux_rows, "row", split_axis=0, concat_axis=0, tiled=True)
    emb_back = lax.all_to_all(emb_rows, "row", split_axis=0, concat_axis=0, tiled=True)
    near_aux = jnp.take(aux_back.reshape(-1, width), entry_slot, axis=0).reshape(
        new_dev, slots_row, width
    )
    near_emb = jnp.take(emb_back.reshape(-1, width), entry_slot, axis=0).reshape(
        new_dev, slots_row, width
    )
    inner = jnp.einsum("jd,jkd->jk", new_aux, near_aux, preferred_element_type=jnp.float32)
    near_sq = jnp.einsum("jkd,jkd->jk", near_aux, near_aux, preferred_element_type=jnp.float32)
    own_sq = jnp.einsum("jd,jd->j", new_aux, new_aux, preferred_element_type=jnp.float32)
    inner, near_sq, own_sq = packed_total((inner, near_sq, own_sq), "col")
    angular_similarity_values = inner * lax.rsqrt((own_sq[:, None] + eps) * (near_sq + eps))
    plain_affinity_values = jnp.where(
        admissible_flags,
        jnp.exp(angular_similarity_values / exponential_sharpness),
        jnp.float32(0.0),
    )
    weights = (
        plain_affinity_values / jnp.sum(plain_affinity_values, axis=1, keepdims=True)
    ).astype(jnp.bfloat16)
    blended = jnp.einsum("jk,jkd->jd", weights, near_emb, preferred_element_type=jnp.float32)
    return blended.astype(jnp.bfloat16)


def solution(mesh):
    return jax.shard_map(
        local,
        mesh=mesh,
        in_specs=(P("row", "col"), P("row", "col"), P("row", "col"), P("row", None), P("row")),
        out_specs=P("row", "col"),
        check_vma=False,
    )
```

profile of v0, /device:TPU:1, one launch (start us, length us, event | category | flops | bytes accessed | tf_op | source)
XLA Modules:
  0.0 207.7 jit_solution(13175735864343796832)
XLA Ops:
  0.0 0.8 fusion.17
  0.8 0.7 broadcast_divide_fusion
  1.5 0.1 copy.48
  1.6 0.1 and.44
  1.7 0.1 and.42
  1.8 0.7 lt.94
  2.6 0.7 iota_compare_fusion.2
  3.3 0.1 lt.91
  3.4 0.1 lt.90
  3.5 0.1 copy.49
  3.6 0.1 div.49
  3.7 0.1 div.47
  3.8 0.8 copy.47
  4.6 0.1 lt.95
  4.7 0.1 lt.96
  4.8 0.1 reshape.270
  4.9 0.1 lt.93
  5.0 18.1 %reduce-window.6 = s32[64,16,128]{2,1,0:T(8,128)S(1)} reduce-window(s32[64,16,128]{2,1,0:T(8,128)S(1)} %fusion.3, s32[]{:T(128)} %constant.14.clone.1), window={size=1x1x128 pad=0_0x0_0x127_0}, to_apply=%region_0.1 | reduce-window | flops 16646144 | bytes 1048580 | tf_op jit(solution)/shard_map/reduce-window
  23.2 0.2 slice.58
  23.4 0.4 copy.71
  23.8 0.2 reduce-window.9
  24.0 0.2 add_add_fusion
  24.2 0.2 fusion.2
  24.5 8.1 %scatter_custom_fusion = s32[3073]{0:T(1024)S(1)} fusion(s32[2048]{0:T(1024)S(1)} %bitcast.65, s32[2048]{0:T(1024)S(1)} %get-tuple-element.16, s32[]{:T(128)} %constant.32.clone.1), kind=kCustom, calls=%fused_computation.60 | custom fusion | bytes 12296 | tf_op jit(solution)/shard_map/scatter | solution.py:42
  32.6 0.1 reshape.272
  32.7 1.0 sort.15
  33.7 0.1 copy.55
  33.8 0.1 reshape.334
  33.9 0.1 fusion.22
  34.0 0.2 reduce_window_sum.25
  34.2 0.1 and_reduce_fusion
  34.3 0.1 multiply_reduce_fusion
  34.4 0.1 reshape.332
  34.5 11.8 %scatter_custom_fusion.1 = s32[1600]{0:T(1024)S(1)} fusion(s32[3072]{0:T(1024)S(1)} %reshape.332, s32[3072]{0:T(1024)S(1)} %reshape.334, s32[]{:T(128)} %constant.32.clone.1), kind=kCustom, calls=%fused_computation.67 | custom fusion | bytes 6404
  46.4 0.1 copy.59
  46.5 27.8 %all_to_all.25 = s32[64,1,24]{2,1,0:T(1,128)S(1)} all-to-all(s32[64,1,24]{2,1,0:T(1,128)S(1)} %bitcast.46), channel_id=1, replica_groups=mesh['row'=64,'col'=8] {'row'}, dimensions={0} | all-to-all | bytes 12288 | tf_op jit(solution)/shard_map/all_to_all | solution.py:62
  74.3 0.1 reshape.344
  74.5 5.4 %gather_fusion.3 = bf16[1536,512]{1,0:T(8,128)(2,1)} fusion(bf16[1280,512]{1,0:T(8,128)(2,1)S(1)} %copy-done, s32[2048]{0:T(1024)S(1)} %pad_clamp_fusion), kind=kCustom, calls=%fused_computation.2.clone | custom fusion | bytes 3151872 | tf_op jit(solution)/shard_map/jit(_take)/gather | solution.py:65
  79.9 5.4 %gather_fusion.1 = bf16[1536,512]{1,0:T(8,128)(2,1)} fusion(bf16[1280,512]{1,0:T(8,128)(2,1)S(1)} %copy-done.1, s32[2048]{0:T(1024)S(1)} %pad_clamp_fusion), kind=kCustom, calls=%fused_computation.clone | custom fusion | bytes 3151872 | tf_op jit(solution)/shard_map/jit(_take)/gather | solution.py:64
  85.3 2.9 %broadcast_select_fusion.3 = (bf16[64,24,512]{2,1,0:T(8,128)(2,1)}, bf16[64,24,512]{2,1,0:T(8,128)(2,1)S(1)}) fusion(bf16[64,24,512]{2,1,0:T(8,128)(2,1)} %bitcast.54, pred[64,24]{1,0:T(8,128)(4,1)S(1)} %compare_and_fusion, bf16[64,24,512]{2,1,0:T(8,128)(2,1)} %bitcast.53), kind=kLoop, calls=%fused_computation.12 | loop fusion | flops 1572864 | bytes 6292992 | tf_op jit(solution)/shard_map/jit(_take)/select_n | solution.py:64
  88.2 41.2 %all_to_all.26 = bf16[64,24,512]{2,1,0:T(8,128)(2,1)} all-to-all(bf16[64,24,512]{2,1,0:T(8,128)(2,1)S(1)} %get-tuple-element.19), channel_id=1, replica_groups=mesh['row'=64,'col'=8] {'row'}, dimensions={0} | all-to-all | bytes 3145728 | tf_op jit(solution)/shard_map/all_to_all | solution.py:67
  129.4 10.8 %all-to-all-start.1 = ((bf16[64,24,512]{2,1,0:T(8,128)(2,1)}), bf16[64,24,512]{2,1,0:T(8,128)(2,1)S(1)}, u32[]{:S(2)}, u32[]{:S(2)}) async-start(bf16[64,24,512]{2,1,0:T(8,128)(2,1)} %get-tuple-element.18), calls=%async_computation.1 | async-start | bytes 3145728 | tf_op jit(solution)/shard_map/all_to_all | solution.py:66
  140.3 7.6 %gather_fusion = s32[2048,24]{1,0:T(8,128)} fusion(s32[64,24]{1,0:T(8,128)S(1)} %bitcast.47, s32[2048]{0:T(1024)S(1)} %broadcast_clamp_fusion.2), kind=kCustom, calls=%fused_computation.4 | custom fusion | bytes 401408 | tf_op jit(solution)/shard_map/gather | solution.py:57
  147.9 0.1 fusion.4
  148.0 1.9 select_reduce_fusion
  149.9 10.8 %gather_fusion.4 = bf16[2048,512]{1,0:T(8,128)(2,1)} fusion(bf16[1536,512]{1,0:T(8,128)(2,1)} %bitcast.49, s32[2048]{0:T(1024)S(1)} %broadcast_clamp_fusion.1), kind=kCustom, calls=%fused_computation.3.clone | custom fusion | bytes 4202496 | tf_op jit(solution)/shard_map/jit(_take)/gather | solution.py:71
  160.7 15.6 %all-to-all-done.1 = bf16[64,24,512]{2,1,0:T(8,128)(2,1)S(1)} async-done(((bf16[64,24,512]{2,1,0:T(8,128)(2,1)}), bf16[64,24,512]{2,1,0:T(8,128)(2,1)S(1)}, u32[]{:S(2)}, u32[]{:S(2)}) %all-to-all-start.1) | async-done | bytes 1572896 | tf_op jit(solution)/shard_map/all_to_all | solution.py:66
  176.3 9.2 %gather_fusion.2 = bf16[2048,512]{1,0:T(8,128)(2,1)} fusion(bf16[1536,512]{1,0:T(8,128)(2,1)S(1)} %bitcast.48, s32[2048]{0:T(1024)S(1)} %broadcast_clamp_fusion.1), kind=kCustom, calls=%fused_computation.1.clone | custom fusion | bytes 4202496 | tf_op jit(solution)/shard_map/jit(_take)/gather | solution.py:68
  185.5 2.5 %broadcast_select_fusion.1 = (bf16[2048,512]{1,0:T(8,128)(2,1)S(1)}, bf16[2048,512]{1,0:T(8,128)(2,1)S(1)}) fusion(bf16[2048,512]{1,0:T(8,128)(2,1)} %gather_fusion.2, pred[2048]{0:T(1024)(128)(4,1)S(1)} %compare_and_fusion.1, bf16[2048,512]{1,0:T(8,128)(2,1)} %gather_fusion.4), kind=kLoop, calls=%fused_computation.10 | loop fusion | flops 2097152 | bytes 8390656 | tf_op jit(solution)/shard_map/jit(_take)/select_n | solution.py:68
  188.0 0.5 fusion
  188.4 0.4 copy-done.3
  188.9 0.7 fusion.5
  189.6 0.1 reshape.276
  189.7 0.1 reshape.275
  189.9 14.1 %all_to_all.27 = f32[8,1,4224]{2,1,0:T(1,128)S(1)} all-to-all(f32[8,1,4224]{2,1,0:T(1,128)S(1)} %broadcast_in_dim.79), channel_id=1, replica_groups=mesh['row'=64,'col'=8] {'col'}, dimensions={0} | all-to-all | bytes 270336 | tf_op jit(solution)/shard_map/all_to_all | solution.py:12
  204.0 0.7 reduce_sum.41
  204.7 0.7 slice_add_fusion.1
  205.4 0.7 slice_add_fusion
  206.1 0.1 add.109
  206.2 0.1 reshape.277
  206.3 0.2 fusion.21
  206.5 0.1 fusion.10
  206.6 0.4 fusion.7
  207.1 0.7 copy.85
  (34 shorter events, 0.5 us)
Async XLA Ops:
  0.0 74.4 %copy-start = (bf16[1280,512]{1,0:T(8,128)(2,1)S(1)}, bf16[1280,512]{1,0:T(8,128)(2,1)}, u32[]{:S(2)}) copy-start(bf16[1280,512]{1,0:T(8,128)(2,1)} %param.11) | copy-start | bytes 3932164
  23.2 11.1 %copy-start.6 = (s32[2]{0:T(128)S(1)}, s32[2]{0:T(128)}, u32[]{:S(2)}) copy-start(s32[2]{0:T(128)} %constant.84) | copy-start | bytes 28
  23.2 11.2 %copy-start.5 = (s32[2]{0:T(128)S(1)}, s32[2]{0:T(128)}, u32[]{:S(2)}) copy-start(s32[2]{0:T(128)} %constant.49) | copy-start | bytes 28
  74.4 5.4 %copy-start.1 = (bf16[1280,512]{1,0:T(8,128)(2,1)S(1)}, bf16[1280,512]{1,0:T(8,128)(2,1)}, u32[]{:S(2)}) copy-start(bf16[1280,512]{1,0:T(8,128)(2,1)} %param.10) | copy-start | bytes 3932164
  129.4 46.9 %all-to-all-start.1 = ((bf16[64,24,512]{2,1,0:T(8,128)(2,1)}), bf16[64,24,512]{2,1,0:T(8,128)(2,1)S(1)}, u32[]{:S(2)}, u32[]{:S(2)}) async-start(bf16[64,24,512]{2,1,0:T(8,128)(2,1)} %get-tuple-element.18), calls=%async_computation.1 | async-start | bytes 3145728 | tf_op jit(solution)/shard_map/all_to_all | solution.py:66
  140.3 7.6 %copy-start.2 = (bf16[128,512]{1,0:T(8,128)(2,1)S(1)}, bf16[128,512]{1,0:T(8,128)(2,1)}, u32[]{:S(2)}) copy-start(bf16[128,512]{1,0:T(8,128)(2,1)} %param.9) | copy-start | bytes 393220
  188.0 0.9 copy-start.3
  188.9 17.4 %copy-start.4 = (s32[128]{0:T(128)S(1)}, s32[128]{0:T(128)}, u32[]{:S(2)}) copy-start(s32[128]{0:T(128)} %param.13) | copy-start | bytes 1540
where the time goes:
time: 209 us; the launch traced here: 208 us
  blocking collectives  83.1 us (40%)
  local copies, waits for them, and re-layouts  63.7 us (30%)
  other arithmetic  33 us (16%)
  waiting for transfers between devices  15.6 us (7%)
  starting transfers between devices  10.8 us (5%)
    all_to_all x1, blocking collectives, local(): lax.all_to_all(emb_rows, 'row', split_axis=0, concat_axis=0, tiled=True)  41.2 us
    all_to_all x1, blocking collectives, local(): lax.all_to_all(compact, 'row', split_axis=0, concat_axis=0, tiled=True)  27.8 us
    another operation x2, other arithmetic  18.3 us
    all_to_all x1, waiting for transfers between devices, local(): lax.all_to_all(aux_rows, 'row', split_axis=0, concat_axis=0, tiled=True)  15.6 us
    all_to_all x1, blocking collectives, sent_to_all(): lax.all_to_all(jnp.broadcast_to(x[None], (length, *x.shape)), axis, 0, 0,...  14.1 us
    unnamed x19, local copies, waits for them, and re-layouts  13.3 us
    all_to_all x1, starting transfers between devices, local(): lax.all_to_all(aux_rows, 'row', split_axis=0, concat_axis=0, tiled=True)  10.8 us
    gather x1, local copies, waits for them, and re-layouts, local(): jnp.take(emb_back.reshape(-1, width), entry_slot, axis=0)  10.8 us
  transfers between devices with their start and end apart: 1, of which 1 were waited for; matrix products, arithmetic and copies ran while one was open for 10% of the time, Pallas kernels for 0%

commit v1 on v0

v1 whole, which is shorter than its diff:
```python
import functools

import jax
import jax.numpy as jnp
from jax import lax
from jax.experimental import pallas as pl
from jax.experimental.pallas import tpu as pltpu
from jax.sharding import PartitionSpec as P

MESH = pl.DeviceIdType.MESH
F32, BF16, I32 = jnp.float32, jnp.bfloat16, jnp.int32
DISTINCT = 24
SIDE = 8
LANES = 128
eps = 1e-06
exponential_sharpness = 0.025


def iota(shape, dim):
    return lax.broadcasted_iota(I32, shape, dim)


def kernel(n_row, n_col, ids_ref, cnt_ref, new_ref, aux_hbm, emb_hbm, out_ref,
           aux_tab, emb_tab, row_hot, lo_hot, ranks, lists, asked, sel, send_aux, send_emb,
           got_aux, got_emb, slot_wide, w_wide, w_slots, part, parts,
           tab_sem, list_send, list_recv, aux_send, aux_recv, emb_send, emb_recv, part_send, part_recv):
    slots_row, new_dev = ids_ref.shape
    old_dev, width = aux_hbm.shape
    his = old_dev // LANES
    me = lax.axis_index("row")
    my_col = lax.axis_index("col")
    y, z = me // SIDE, me % SIDE

    def shift(i):
        p, q = i % SIDE, i // SIDE
        return (3 * p) % SIDE, (3 * q + p) % SIDE

    def asker(i):
        dy, dz = shift(i)
        return ((y + dy) % SIDE) * SIDE + (z + dz) % SIDE

    def owner(i):
        dy, dz = shift(i)
        return ((y - dy + SIDE) % SIDE) * SIDE + (z - dz + SIDE) % SIDE

    tabs = [pltpu.make_async_copy(aux_hbm, aux_tab, tab_sem.at[0]),
            pltpu.make_async_copy(emb_hbm, emb_tab, tab_sem.at[1])]
    for t in tabs:
        t.start()

    barrier = pltpu.get_barrier_semaphore()

    def greet(i, c):
        pl.semaphore_signal(barrier, inc=1, device_id={"row": asker(i)}, device_id_type=MESH)
        return c
    lax.fori_loop(1, n_row, greet, 0)
    for c in range(1, n_col):
        pl.semaphore_signal(barrier, inc=1, device_id={"col": (my_col + c) % n_col}, device_id_type=MESH)

    ids = ids_ref[...]
    live = iota(ids.shape, 0) < cnt_ref[...]
    group = jnp.where(live, ids, 0) >> 7
    lo = ids & (LANES - 1)
    own = (group * 205) >> 11
    hi = group - his * own
    at = jnp.where(live, hi * n_row + own, -1)
    sub_all = iota((his * n_row, new_dev), 0)
    sub_lo = iota((LANES, new_dev), 0)
    for k in range(slots_row):
        cols = slice(k * new_dev, (k + 1) * new_dev)
        row_hot[:, cols] = jnp.where(sub_all == at[k:k + 1, :], 1.0, 0.0).astype(BF16)
        lo_hot[:, cols] = jnp.where(sub_lo == lo[k:k + 1, :], 1.0, 0.0).astype(BF16)
    named = lax.dot_general(row_hot[...], lo_hot[...], (((1,), (1,)), ((), ())), preferred_element_type=F32)
    present = named > 0.5
    mask = jnp.where(present, 1.0, 0.0).astype(BF16)
    i0, i1 = iota((LANES, LANES), 0), iota((LANES, LANES), 1)
    before = jnp.dot(mask, jnp.where(i0 < i1, 1.0, 0.0).astype(BF16), preferred_element_type=F32)
    per_row = jnp.dot(mask, jnp.ones((LANES, LANES), BF16), preferred_element_type=F32)
    ahead = jnp.zeros((n_row, LANES), F32)
    for h in range(his):
        rows = slice(h * n_row, (h + 1) * n_row)
        ranks[rows, :] = jnp.where(present[rows], before[rows] + ahead, -1.0)
        ahead = ahead + per_row[rows]

    lane = iota((n_row, LANES), 1)
    lane_f = lane.astype(F32)
    table = jnp.zeros((n_row, LANES), F32)
    for c in range(DISTINCT):
        acc = jnp.zeros((n_row, LANES), F32)
        for h in range(his):
            acc = acc + jnp.where(ranks[h * n_row:(h + 1) * n_row, :] == float(c), lane_f + float(h * LANES), 0.0)
        table = jnp.where(lane == c, jnp.sum(acc, axis=1, keepdims=True), table)
    for o in range(n_row):
        lists[o] = table[o:o + 1, :]

    pl.semaphore_wait(barrier, n_row - 1 + n_col - 1)

    groups = list_recv.shape[0]
    per = n_row // groups
    pltpu.make_async_copy(lists.at[me], asked.at[0], list_recv.at[0]).start()

    def ask(i, c):
        pltpu.make_async_remote_copy(
            lists.at[me * 0 + owner(i)], asked.at[i], list_send, list_recv.at[i // per],
            device_id={"row": owner(i)}, device_id_type=MESH).start()
        return c
    lax.fori_loop(1, n_row, ask, 0)

    for t in tabs:
        t.wait()

    wide = iota((DISTINCT, old_dev), 1).astype(F32)

    def send(src, dst, s_sem, r_sem, i):
        return pltpu.make_async_remote_copy(src.at[i], dst.at[me], s_sem, r_sem,
                                            device_id={"row": asker(i)}, device_id_type=MESH)

    def put(g, tab, src, dst, s_sem, r_sem):
        rows = jnp.dot(sel[g * per * DISTINCT:(g + 1) * per * DISTINCT, :], tab[...], preferred_element_type=F32)
        for a in range(per):
            src[g * per + a] = rows[a * DISTINCT:(a + 1) * DISTINCT].astype(BF16)
        if g == 0:
            pltpu.make_async_copy(src.at[0], dst.at[me], r_sem).start()

        def go(i, c):
            send(src, dst, s_sem, r_sem, i).start()
            return c
        lax.fori_loop(max(g * per, 1), (g + 1) * per, go, 0)

    for g in range(groups):
        pltpu.make_async_copy(asked.at[pl.ds(g * per, per)], asked.at[pl.ds(g * per, per)], list_recv.at[g]).wait()
        want = jnp.concatenate([asked[g * per + a] for a in range(per)], axis=0).T
        for a in range(0, per, 2):
            pair = jnp.concatenate(
                [jnp.where(want[:DISTINCT, b:b + 1] == wide, 1.0, 0.0) for b in (a, a + 1)], axis=0)
            sel[(g * per + a) * DISTINCT:(g * per + a + 2) * DISTINCT, :] = pair.astype(BF16)
        put(g, aux_tab, send_aux, got_aux, aux_send, aux_recv)
    for g in range(groups):
        put(g, emb_tab, send_emb, got_emb, emb_send, emb_recv)

    found = lax.dot_general(ranks[...].astype(BF16), row_hot[...], (((0,), (0,)), ((), ())), preferred_element_type=F32)
    for k in range(slots_row):
        cols = slice(k * new_dev, (k + 1) * new_dev)
        pos = jnp.sum(jnp.where(sub_lo == lo[k:k + 1, :], found[:, cols], 0.0), axis=0, keepdims=True)
        slot = jnp.where(live[k:k + 1, :], own[k:k + 1, :] * DISTINCT + pos.astype(I32), -1)
        slot_wide[k] = jnp.broadcast_to(slot, (8, new_dev))

    new = new_ref[...]
    own_sq = jnp.sum(jnp.square(new.astype(F32)), axis=1, keepdims=True)
    own_sq = jnp.broadcast_to(own_sq, (new_dev, LANES)).T[0:8, :]

    pltpu.make_async_copy(got_aux, got_aux, aux_recv).wait()

    sub8 = iota((8, new_dev), 0)

    def inner_step(o, acc):
        rows = got_aux[o]
        prod = lax.dot_general(rows, new, (((1,), (1,)), ((), ())), preferred_element_type=F32)
        near = jnp.broadcast_to(jnp.sum(jnp.square(rows.astype(F32)), axis=1, keepdims=True), (DISTINCT, new_dev))
        acc = list(acc)
        for t in range(DISTINCT // 8):
            here = sub8 + (o * DISTINCT + 8 * t)
            for k in range(slots_row):
                hit = slot_wide[k] == here
                acc[k] = acc[k] + jnp.where(hit, prod[8 * t:8 * t + 8], 0.0)
                acc[slots_row + k] = acc[slots_row + k] + jnp.where(hit, near[8 * t:8 * t + 8], 0.0)
        return tuple(acc)

    acc = lax.fori_loop(0, n_row, inner_step, tuple(jnp.zeros((8, new_dev), F32) for _ in range(2 * slots_row)))
    for k in range(2 * slots_row):
        part[k:k + 1, :] = jnp.sum(acc[k], axis=0, keepdims=True)
    part[2 * slots_row:2 * slots_row + 8, :] = own_sq

    for c in range(1, n_col):
        pltpu.make_async_remote_copy(part, parts.at[c - 1], part_send.at[c - 1], part_recv.at[c - 1],
                                     device_id={"col": (my_col + c) % n_col}, device_id_type=MESH).start()
    total = part[...]
    for c in range(1, n_col):
        pltpu.make_async_copy(part, parts.at[c - 1], part_recv.at[c - 1]).wait()
        total = total + parts[c - 1]

    inner, near_sq = total[:slots_row], total[slots_row:2 * slots_row]
    own_all = total[2 * slots_row:2 * slots_row + 1]
    similarity = inner * lax.rsqrt((own_all + eps) * (near_sq + eps))
    raw = jnp.where(live, jnp.exp(similarity / exponential_sharpness), 0.0)
    weights = (raw / jnp.sum(raw, axis=0, keepdims=True)).astype(BF16).astype(F32)
    for k in range(slots_row):
        w_wide[k] = jnp.broadcast_to(weights[k:k + 1, :], (8, new_dev))

    def weigh(o, c):
        for t in range(DISTINCT // 8):
            start = pl.multiple_of(o * DISTINCT + 8 * t, 8)
            here = sub8 + start
            acc = jnp.zeros((8, new_dev), F32)
            for k in range(slots_row):
                acc = acc + jnp.where(slot_wide[k] == here, w_wide[k], 0.0)
            w_slots[pl.ds(start, 8), :] = acc
        return c
    lax.fori_loop(0, n_row, weigh, 0)
    w_t = w_slots[...].T.astype(BF16)

    pltpu.make_async_copy(got_emb, got_emb, emb_recv).wait()
    near_emb = got_emb[...].reshape(n_row * DISTINCT, width)
    out_ref[...] = jnp.dot(w_t, near_emb, preferred_element_type=F32).astype(BF16)

    rest = pl.ds(0, n_row - 1)
    pltpu.make_async_copy(lists.at[rest], lists.at[rest], list_send).wait()
    pltpu.make_async_copy(send_aux.at[rest], send_aux.at[rest], aux_send).wait()
    pltpu.make_async_copy(send_emb.at[rest], send_emb.at[rest], emb_send).wait()
    for c in range(1, n_col):
        pltpu.make_async_copy(part, part, part_send.at[c - 1]).wait()


def solution(mesh):
    n_row, n_col = mesh.shape["row"], mesh.shape["col"]

    def local(new_aux, former_auxiliary_rows, old_emb, neighbour_ids, neighbour_counts):
        new_dev, width = new_aux.shape
        old_dev = former_auxiliary_rows.shape[0]
        slots_row = neighbour_ids.shape[1]
        slots = n_row * DISTINCT
        his = old_dev // LANES
        vm = pltpu.VMEM
        dma = pltpu.SemaphoreType.DMA
        spec = pl.BlockSpec(memory_space=vm)
        hbm = pl.BlockSpec(memory_space=pl.ANY)
        return pl.pallas_call(
            functools.partial(kernel, n_row, n_col),
            out_shape=jax.ShapeDtypeStruct((new_dev, width), BF16),
            in_specs=[spec, spec, spec, hbm, hbm],
            out_specs=spec,
            scratch_shapes=[
                vm((old_dev, width), BF16), vm((old_dev, width), BF16),
                vm((his * n_row, slots_row * new_dev), BF16), vm((LANES, slots_row * new_dev), BF16),
                vm((his * n_row, LANES), F32), vm((n_row, 1, LANES), F32), vm((n_row, 1, LANES), F32),
                vm((slots, old_dev), BF16),
                vm((n_row, DISTINCT, width), BF16), vm((n_row, DISTINCT, width), BF16),
                vm((n_row, DISTINCT, width), BF16), vm((n_row, DISTINCT, width), BF16),

                vm((slots_row, 8, new_dev), I32), vm((slots_row, 8, new_dev), F32),
                vm((slots, new_dev), F32),
                vm((2 * slots_row + 8, new_dev), F32), vm((n_col - 1, 2 * slots_row + 8, new_dev), F32),
                dma((2,)), dma(()), dma((4,)), dma(()), dma(()), dma(()), dma(()),
                dma((n_col - 1,)), dma((n_col - 1,)),
            ],
            compiler_params=pltpu.CompilerParams(
                collective_id=0, has_side_effects=True, vmem_limit_bytes=48 * 1024 * 1024),
        )(neighbour_ids.T, neighbour_counts.reshape(1, new_dev), new_aux, former_auxiliary_rows, old_emb)

    return jax.shard_map(
        local,
        mesh=mesh,
        in_specs=(P("row", "col"), P("row", "col"), P("row", "col"), P("row", None), P("row")),
        out_specs=P("row", "col"),
        check_vma=False,
    )
```

time: 209 us -> 107 us (0.51)
  Pallas kernels: 0 us -> 101 us
  blocking collectives: 83.1 us -> 0 us
  local copies, waits for them, and re-layouts: 63.7 us -> 5.54 us
  other arithmetic: 33 us -> 0 us
  waiting for transfers between devices: 15.6 us -> 0 us
  starting transfers between devices: 10.8 us -> 0 us
    pallas_call x0 -> x1, Pallas kernels: none -> 101 us  [local(): pl.pallas_call(functools.partial(kernel, n_row, n_col), out_shape=jax.Sha...]
    all_to_all x3 -> x0, blocking collectives: 83.1 us -> none  [the longest x1 41.2 us: local(): lax.all_to_all(emb_rows, 'row', split_axis=0, concat_axis=0, tiled=True)]
    gather x5 -> x0, local copies, waits for them, and re-layouts: 38.4 us -> none  [the longest x1 10.8 us: local(): jnp.take(emb_back.reshape(-1, width), entry_slot, axis=0)]
    another operation x3 -> x0, other arithmetic: 18.5 us -> none
    all_to_all x1 -> x0, waiting for transfers between devices: 15.6 us -> none  [local(): lax.all_to_all(aux_rows, 'row', split_axis=0, concat_axis=0, tiled=True)]
    all_to_all x1 -> x0, starting transfers between devices: 10.8 us -> none  [local(): lax.all_to_all(aux_rows, 'row', split_axis=0, concat_axis=0, tiled=True)]
    scatter x1 -> x0, local copies, waits for them, and re-layouts: 8.06 us -> none  [local(): jnp.full((devices * capacity + 1,), -1, jnp.int32).at[slots].set(local_rows)]
    unnamed x19 -> x11, local copies, waits for them, and re-layouts: 13.3 us -> 5.54 us
  transfers between devices with their start and end apart: 1 -> 0, of which waited for: 1 -> 0; matrix products, arithmetic and copies ran while one was open for 10% -> 0% of each run, Pallas kernels for 0% -> 0%
where the time goes in v1:
time: 107 us; the launch traced here: 106 us
  Pallas kernels  101 us (94%)
  local copies, waits for them, and re-layouts  5.54 us (5%)
    pallas_call x1, Pallas kernels, local(): pl.pallas_call(functools.partial(kernel, n_row, n_col), out_shape=jax.Sha...  101 us
    unnamed x11, local copies, waits for them, and re-layouts  5.54 us

profile of v1, /device:TPU:1, one launch (start us, length us, event | category | flops | bytes accessed | tf_op | source)
XLA Modules:
  0.0 106.3 jit_solution(6448479194375075340)
XLA Ops:
  0.0 0.0 copy-start
  0.0 1.3 %copy-done = bf16[1280,512]{1,0:T(8,128)(2,1)S(1)} copy-done((bf16[1280,512]{1,0:T(8,128)(2,1)S(1)}, bf16[1280,512]{1,0:T(8,128)(2,1)}, u32[]{:S(2)}) %copy-start) | copy-done | bytes 1310744
  1.3 0.0 copy-start.1
  1.3 1.3 %copy-done.1 = bf16[1280,512]{1,0:T(8,128)(2,1)S(1)} copy-done((bf16[1280,512]{1,0:T(8,128)(2,1)S(1)}, bf16[1280,512]{1,0:T(8,128)(2,1)}, u32[]{:S(2)}) %copy-start.1) | copy-done | bytes 1310744
  2.6 0.0 copy-start.2
  2.6 0.9 copy-done.2
  3.5 0.0 copy-start.3
  3.5 0.7 copy-done.3
  4.2 0.0 copy-start.4
  4.2 0.7 copy-done.4
  4.9 100.7 %shard_map.55 = bf16[128,512]{1,0:T(8,128)(2,1)S(1)} custom-call(s32[16,128]{1,0:T(8,128)S(1)} %bitcast.2, s32[1,128]{1,0:T(1,128)S(1)} %bitcast.3, bf16[128,512]{1,0:T(8,128)(2,1)S(1)} %copy-done.2, bf16[1280,512]{1,0:T(8,128)(2,1)S(1)} %copy-done, bf16[1280,512]{1,0:T(8,128)(2,1)S(1)} %copy-done.1), custom_call_target="tpu_custom_call" | custom-call | tf_op jit(solution)/shard_map/pallas_call | solution.py:227
  105.6 0.7 copy.7
Async XLA Ops:
  0.0 1.3 %copy-start = (bf16[1280,512]{1,0:T(8,128)(2,1)S(1)}, bf16[1280,512]{1,0:T(8,128)(2,1)}, u32[]{:S(2)}) copy-start(bf16[1280,512]{1,0:T(8,128)(2,1)} %aux_hbm.1) | copy-start | bytes 3932164
  1.3 1.3 %copy-start.1 = (bf16[1280,512]{1,0:T(8,128)(2,1)S(1)}, bf16[1280,512]{1,0:T(8,128)(2,1)}, u32[]{:S(2)}) copy-start(bf16[1280,512]{1,0:T(8,128)(2,1)} %emb_hbm.1) | copy-start | bytes 3932164
  2.6 0.9 copy-start.2
  3.5 0.7 copy-start.3
  4.2 0.7 copy-start.4

commit v2 on v1

v2 whole, which is shorter than its diff:
```python
import functools

import jax
import jax.numpy as jnp
from jax import lax
from jax.experimental import pallas as pl
from jax.experimental.pallas import tpu as pltpu
from jax.sharding import PartitionSpec as P

MESH = pl.DeviceIdType.MESH
F32, BF16, I32 = jnp.float32, jnp.bfloat16, jnp.int32
DISTINCT = 24
SIDE = 8
LANES = 128
HOPS = (4, 3, 5, 2, 6, 1, 7, 0)
EARLY = 2
eps = 1e-06
exponential_sharpness = 0.025


def iota(shape, dim):
    return lax.broadcasted_iota(I32, shape, dim)


def total_of(ref, sem):
    return pltpu.make_async_copy(ref, ref, sem)


def kernel(n_row, n_col, ids_hbm, cnt_hbm, new_hbm, aux_hbm, emb_hbm, out_ref,
           ids_ref, cnt_ref, new_all, aux_tab, emb_tab, row_hot, lo_hot, ranks, lists, asked, sel,
           send_aux, send_emb, got_aux, got_emb, code_own, codes, slot_wide, w_wide, w_slots,
           met, gath, part, parts,
           tab_sem, list_send, list_recv, new_send, new_recv, code_send, code_recv, aux_send, aux_recv,
           emb_send, emb_recv, met_send, met_recv, part_send, part_recv):
    slots_row, new_dev = ids_ref.shape
    old_dev, width = aux_hbm.shape
    his = old_dev // LANES
    line = SIDE * DISTINCT
    me = lax.axis_index("row")
    my_col = lax.axis_index("col")
    core = lax.rem(my_col, 2)
    u_step = SIDE - (SIDE - 1) * core
    v_step = SIDE + 1 - u_step
    y, z = lax.div(me, SIDE), lax.rem(me, SIDE)
    u = y + (z - y) * core
    v = z + (y - z) * core

    def at_row(uu, vv):
        return {"row": uu * u_step + vv * v_step}

    def plus(a, d):
        return lax.rem(a + (d % SIDE), SIDE)

    loads = [pltpu.make_async_copy(ids_hbm, ids_ref, tab_sem.at[0]),
             pltpu.make_async_copy(cnt_hbm, cnt_ref, tab_sem.at[1]),
             pltpu.make_async_copy(new_hbm, new_all.at[u], tab_sem.at[2]),
             pltpu.make_async_copy(aux_hbm, aux_tab, tab_sem.at[3]),
             pltpu.make_async_copy(emb_hbm, emb_tab, tab_sem.at[4])]
    for t in loads:
        t.start()

    barrier = pltpu.get_barrier_semaphore()
    for dv in range(SIDE):
        for du in range(SIDE):
            if (du, dv) != (0, 0):
                pl.semaphore_signal(barrier, inc=1, device_id=at_row(plus(u, du), plus(v, dv)), device_id_type=MESH)
    for c in range(1, n_col):
        pl.semaphore_signal(barrier, inc=1, device_id={"col": lax.rem(my_col + c, n_col)}, device_id_type=MESH)

    loads[0].wait()
    loads[1].wait()
    ids = ids_ref[...]
    live = iota(ids.shape, 0) < cnt_ref[...]
    group = jnp.where(live, ids, 0) >> 7
    lo = ids & (LANES - 1)
    own = (group * 205) >> 11
    hi = group - his * own
    at = jnp.where(live, hi * n_row + own, -1)
    sub_all = iota((his * n_row, new_dev), 0)
    sub_lo = iota((LANES, new_dev), 0)
    for k in range(slots_row):
        cols = slice(k * new_dev, (k + 1) * new_dev)
        row_hot[:, cols] = jnp.where(sub_all == at[k:k + 1, :], 1.0, 0.0).astype(BF16)
        lo_hot[:, cols] = jnp.where(sub_lo == lo[k:k + 1, :], 1.0, 0.0).astype(BF16)
    named = lax.dot_general(row_hot[...], lo_hot[...], (((1,), (1,)), ((), ())), preferred_element_type=F32)
    present = named > 0.5
    mask = jnp.where(present, 1.0, 0.0).astype(BF16)
    i0, i1 = iota((LANES, LANES), 0), iota((LANES, LANES), 1)
    before = jnp.dot(mask, jnp.where(i0 < i1, 1.0, 0.0).astype(BF16), preferred_element_type=F32)
    per_row = jnp.dot(mask, jnp.ones((LANES, LANES), BF16), preferred_element_type=F32)
    ahead = jnp.zeros((n_row, LANES), F32)
    for h in range(his):
        rows = slice(h * n_row, (h + 1) * n_row)
        ranks[rows, :] = jnp.where(present[rows], before[rows] + ahead, -1.0)
        ahead = ahead + per_row[rows]

    lane = iota((n_row, LANES), 1)
    lane_f = lane.astype(F32)
    table = jnp.zeros((n_row, LANES), F32)
    for c in range(DISTINCT):
        acc = jnp.zeros((n_row, LANES), F32)
        for h in range(his):
            acc = acc + jnp.where(ranks[h * n_row:(h + 1) * n_row, :] == float(c), lane_f + float(h * LANES), 0.0)
        table = jnp.where(lane == c, jnp.sum(acc, axis=1, keepdims=True), table)
    for o in range(n_row):
        lists[o] = table[o:o + 1, :]

    pl.semaphore_wait(barrier, n_row - 1 + n_col - 1)

    for dv in HOPS:
        for du in range(SIDE):
            uu, vv = plus(u, -du), plus(v, -dv)
            mine = lists.at[uu * u_step + vv * v_step]
            if (du, dv) == (0, 0):
                pltpu.make_async_copy(mine, asked.at[0, u], list_recv.at[0]).start()
            else:
                pltpu.make_async_remote_copy(mine, asked.at[dv, u], list_send, list_recv.at[dv],
                                             device_id=at_row(uu, vv), device_id_type=MESH).start()

    loads[2].wait()
    for du in (4, 3, 5, 2, 6, 1, 7):
        pltpu.make_async_remote_copy(new_all.at[u], new_all.at[u], new_send, new_recv,
                                     device_id=at_row(plus(u, du), v), device_id_type=MESH).start()

    found = lax.dot_general(ranks[...].astype(BF16), row_hot[...], (((0,), (0,)), ((), ())), preferred_element_type=F32)
    own_y, own_z = own >> 3, own & (SIDE - 1)
    own_uv = (own_y + (own_z - own_y) * core) * SIDE + own_z + (own_y - own_z) * core
    for k in range(slots_row):
        cols = slice(k * new_dev, (k + 1) * new_dev)
        pos = jnp.sum(jnp.where(sub_lo == lo[k:k + 1, :], found[:, cols], 0.0), axis=0, keepdims=True)
        code_own[k:k + 1, :] = jnp.where(live[k:k + 1, :], own_uv[k:k + 1, :] * DISTINCT + pos.astype(I32), -1)
    pltpu.make_async_copy(code_own, codes.at[u], code_recv).start()
    for du in (4, 3, 5, 2, 6, 1, 7):
        pltpu.make_async_remote_copy(code_own, codes.at[u], code_send, code_recv,
                                     device_id=at_row(plus(u, du), v), device_id_type=MESH).start()

    loads[3].wait()
    loads[4].wait()

    wide = iota((DISTINCT, old_dev), 1).astype(F32)

    def gather(dv, tab, dst):
        rows = jnp.dot(sel[dv * line:(dv + 1) * line, :], tab[...], preferred_element_type=F32)
        for a in range(SIDE):
            dst[dv, a] = rows[a * DISTINCT:(a + 1) * DISTINCT].astype(BF16)

    for dv in HOPS:
        total_of(asked.at[dv], list_recv.at[dv]).wait()
        want = jnp.concatenate([asked[dv, a] for a in range(SIDE)], axis=0).T
        for a in range(0, SIDE, 2):
            pair = jnp.concatenate(
                [jnp.where(want[:DISTINCT, b:b + 1] == wide, 1.0, 0.0) for b in (a, a + 1)], axis=0)
            sel[dv * line + a * DISTINCT:dv * line + (a + 2) * DISTINCT, :] = pair.astype(BF16)
        gather(dv, aux_tab, send_aux)
        if dv == 0:
            pltpu.make_async_copy(send_aux.at[0], got_aux.at[v], aux_recv).start()
        else:
            pltpu.make_async_remote_copy(send_aux.at[dv], got_aux.at[v], aux_send, aux_recv,
                                         device_id=at_row(u, plus(v, dv)), device_id_type=MESH).start()
    for dv in HOPS:
        gather(dv, emb_tab, send_emb)

    def send_line(dv):
        for du in (4, 3, 5, 2, 6, 1, 7, 0):
            uu, vv = plus(u, du), plus(v, dv)
            if (du, dv) == (0, 0):
                pltpu.make_async_copy(send_emb.at[0, u], got_emb.at[u * SIDE + v], emb_recv).start()
            else:
                pltpu.make_async_remote_copy(send_emb.at[dv, uu], got_emb.at[u * SIDE + v], emb_send, emb_recv,
                                             device_id=at_row(uu, vv), device_id_type=MESH).start()

    total_of(send_aux.at[pl.ds(0, SIDE - 1)], aux_send).wait()
    for dv in HOPS[:EARLY]:
        send_line(dv)

    own_sq = jnp.sum(jnp.square(new_all[u].astype(F32)), axis=1, keepdims=True)
    part[2 * slots_row:2 * slots_row + 8, :] = jnp.broadcast_to(own_sq, (new_dev, LANES)).T[0:8, :]

    total_of(new_all.at[pl.ds(0, SIDE - 1)], new_recv).wait()
    total_of(codes, code_recv).wait()
    total_of(got_aux, aux_recv).wait()

    sub8 = iota((8, new_dev), 0)

    def meet(a, carry):
        new = new_all[a]
        acc = [jnp.zeros((8, new_dev), F32) for _ in range(2 * slots_row)]
        code = codes[a] - u * line
        rows = jnp.concatenate([got_aux[b, a] for b in range(SIDE)], axis=0)
        prod = lax.dot_general(rows, new, (((1,), (1,)), ((), ())), preferred_element_type=F32)
        near = jnp.broadcast_to(jnp.sum(jnp.square(rows.astype(F32)), axis=1, keepdims=True), (line, new_dev))
        for t in range(line // 8):
            here = sub8 + 8 * t
            for k in range(slots_row):
                hit = code[k:k + 1, :] == here
                acc[k] = acc[k] + jnp.where(hit, prod[8 * t:8 * t + 8], 0.0)
                acc[slots_row + k] = acc[slots_row + k] + jnp.where(hit, near[8 * t:8 * t + 8], 0.0)
        for k in range(2 * slots_row):
            met[a, k:k + 1, :] = jnp.sum(acc[k], axis=0, keepdims=True)
        return carry

    lax.fori_loop(0, SIDE, meet, 0)
    for du in (4, 3, 5, 2, 6, 1, 7, 0):
        uu = plus(u, du)
        if du == 0:
            pltpu.make_async_copy(met.at[u], gath.at[u], met_recv).start()
        else:
            pltpu.make_async_remote_copy(met.at[uu], gath.at[u], met_send, met_recv,
                                         device_id=at_row(uu, v), device_id_type=MESH).start()
    for dv in HOPS[EARLY:]:
        send_line(dv)

    for k in range(slots_row):
        slot_wide[k] = jnp.broadcast_to(code_own[k:k + 1, :], (8, new_dev))
    total_of(gath, met_recv).wait()
    both = gath[0]
    for a in range(1, SIDE):
        both = both + gath[a]
    part[0:2 * slots_row, :] = both
    for c in range(1, n_col):
        pltpu.make_async_remote_copy(part, parts.at[c - 1], part_send, part_recv,
                                     device_id={"col": lax.rem(my_col + c, n_col)}, device_id_type=MESH).start()
    total = part[...]
    total_of(parts, part_recv).wait()
    for c in range(1, n_col):
        total = total + parts[c - 1]

    inner, near_sq = total[:slots_row], total[slots_row:2 * slots_row]
    own_all = total[2 * slots_row:2 * slots_row + 1]
    similarity = inner * lax.rsqrt((own_all + eps) * (near_sq + eps))
    raw = jnp.where(live, jnp.exp(similarity / exponential_sharpness), 0.0)
    weights = (raw / jnp.sum(raw, axis=0, keepdims=True)).astype(BF16).astype(F32)
    for k in range(slots_row):
        w_wide[k] = jnp.broadcast_to(weights[k:k + 1, :], (8, new_dev))

    def weigh(o, c):
        for t in range(DISTINCT // 8):
            start = pl.multiple_of(o * DISTINCT + 8 * t, 8)
            here = sub8 + start
            acc = jnp.zeros((8, new_dev), F32)
            for k in range(slots_row):
                acc = acc + jnp.where(slot_wide[k] == here, w_wide[k], 0.0)
            w_slots[pl.ds(start, 8), :] = acc
        return c
    lax.fori_loop(0, n_row, weigh, 0)
    w_t = w_slots[...].T.astype(BF16)

    total_of(got_emb, emb_recv).wait()
    near_emb = got_emb[...].reshape(n_row * DISTINCT, width)
    out_ref[...] = jnp.dot(w_t, near_emb, preferred_element_type=F32).astype(BF16)

    total_of(lists.at[pl.ds(0, n_row - 1)], list_send).wait()
    total_of(new_all.at[pl.ds(0, SIDE - 1)], new_send).wait()
    total_of(codes.at[pl.ds(0, SIDE - 1)], code_send).wait()
    total_of(got_emb.at[pl.ds(0, n_row - 1)], emb_send).wait()
    total_of(met.at[pl.ds(0, SIDE - 1)], met_send).wait()
    total_of(parts, part_send).wait()


def solution(mesh):
    n_row, n_col = mesh.shape["row"], mesh.shape["col"]

    def local(new_aux, former_auxiliary_rows, old_emb, neighbour_ids, neighbour_counts):
        new_dev, width = new_aux.shape
        old_dev = former_auxiliary_rows.shape[0]
        slots_row = neighbour_ids.shape[1]
        slots = n_row * DISTINCT
        his = old_dev // LANES
        vm = pltpu.VMEM
        dma = pltpu.SemaphoreType.DMA
        hbm = pl.BlockSpec(memory_space=pl.ANY)
        return pl.pallas_call(
            functools.partial(kernel, n_row, n_col),
            out_shape=jax.ShapeDtypeStruct((new_dev, width), BF16),
            in_specs=[hbm] * 5,
            out_specs=pl.BlockSpec(memory_space=vm),
            scratch_shapes=[
                vm((slots_row, new_dev), I32), vm((1, new_dev), I32), vm((SIDE, new_dev, width), BF16),
                vm((old_dev, width), BF16), vm((old_dev, width), BF16),
                vm((his * n_row, slots_row * new_dev), BF16), vm((LANES, slots_row * new_dev), BF16),
                vm((his * n_row, LANES), F32), vm((n_row, 1, LANES), F32), vm((SIDE, SIDE, 1, LANES), F32),
                vm((slots, old_dev), BF16),
                vm((SIDE, SIDE, DISTINCT, width), BF16), vm((SIDE, SIDE, DISTINCT, width), BF16),
                vm((SIDE, SIDE, DISTINCT, width), BF16), vm((n_row, DISTINCT, width), BF16),
                vm((slots_row, new_dev), I32), vm((SIDE, slots_row, new_dev), I32),
                vm((slots_row, 8, new_dev), I32), vm((slots_row, 8, new_dev), F32),
                vm((slots, new_dev), F32),
                vm((SIDE, 2 * slots_row, new_dev), F32), vm((SIDE, 2 * slots_row, new_dev), F32),
                vm((2 * slots_row + 8, new_dev), F32), vm((n_col - 1, 2 * slots_row + 8, new_dev), F32),
                dma((5,)), dma(()), dma((SIDE,)), dma(()), dma(()), dma(()), dma(()), dma(()), dma(()),
                dma(()), dma(()), dma(()), dma(()), dma(()), dma(()),
            ],
            compiler_params=pltpu.CompilerParams(
                collective_id=0, has_side_effects=True, vmem_limit_bytes=67043328),
        )(neighbour_ids.T, neighbour_counts.reshape(1, new_dev), new_aux, former_auxiliary_rows, old_emb)

    return jax.shard_map(
        local,
        mesh=mesh,
        in_specs=(P("row", "col"), P("row", "col"), P("row", "col"), P("row", None), P("row")),
        out_specs=P("row", "col"),
        check_vma=False,
    )
```

time: 107 us -> 100 us (0.935)
  local copies, waits for them, and re-layouts: 5.54 us -> 1.57 us
  Pallas kernels: 101 us -> 98.3 us
    unnamed x11 -> x1, local copies, waits for them, and re-layouts: 5.54 us -> 1.57 us
    pallas_call x1, Pallas kernels: 101 us -> 98.3 us  [local(): pl.pallas_call(functools.partial(kernel, n_row, n_col), out_shape=jax.Sha...]
where the time goes in v2:
time: 100 us; the launch traced here: 99.9 us
  Pallas kernels  98.3 us (98%)
  local copies, waits for them, and re-layouts  1.57 us (2%)
    pallas_call x1, Pallas kernels, local(): pl.pallas_call(functools.partial(kernel, n_row, n_col), out_shape=jax.Sha...  98.3 us

profile of v2, /device:TPU:1, one launch (start us, length us, event | category | flops | bytes accessed | tf_op | source)
XLA Modules:
  0.0 99.9 jit_solution(11772558262760426984)
XLA Ops:
  0.0 98.3 %shard_map.55 = bf16[128,512]{1,0:T(8,128)(2,1)} custom-call(s32[16,128]{1,0:T(8,128)} %bitcast.2, s32[1,128]{1,0:T(1,128)} %bitcast.3, bf16[128,512]{1,0:T(8,128)(2,1)} %new_hbm.1, bf16[1280,512]{1,0:T(8,128)(2,1)} %aux_hbm.1, bf16[1280,512]{1,0:T(8,128)(2,1)} %emb_hbm.1), custom_call_target="tpu_custom_call" | custom-call | tf_op jit(solution)/shard_map/pallas_call | solution.py:272
  98.3 1.6 %copy.7 = bf16[128,512]{1,0:T(8,128)(2,1)} copy(bf16[128,512]{1,0:T(8,128)(2,1)} %shard_map.55) | data formatting | bytes 262144

commit v3 on v2

--- a/solution.py
+++ b/solution.py
@@ -60,8 +60,8 @@
         t.start()
 
     barrier = pltpu.get_barrier_semaphore()
-    for dv in range(SIDE):
-        for du in range(SIDE):
+    for dv in HOPS:
+        for du in HOPS:
             if (du, dv) != (0, 0):
                 pl.semaphore_signal(barrier, inc=1, device_id=at_row(plus(u, du), plus(v, dv)), device_id_type=MESH)
     for c in range(1, n_col):
@@ -108,7 +108,7 @@
     pl.semaphore_wait(barrier, n_row - 1 + n_col - 1)
 
     for dv in HOPS:
-        for du in range(SIDE):
+        for du in HOPS:
             uu, vv = plus(u, -du), plus(v, -dv)
             mine = lists.at[uu * u_step + vv * v_step]
             if (du, dv) == (0, 0):
@@ -117,18 +117,30 @@
                 pltpu.make_async_remote_copy(mine, asked.at[dv, u], list_send, list_recv.at[dv],
                                              device_id=at_row(uu, vv), device_id_type=MESH).start()
 
+    def hand(block, du):
+        src = new_all.at[plus(u, -block)]
+        pltpu.make_async_remote_copy(src, src, new_send, new_recv.at[(block + du) % SIDE],
+                                     device_id=at_row(plus(u, du), v), device_id_type=MESH).start()
+
+    def block_in(block):
+        total_of(new_all.at[plus(u, -block)], new_recv.at[block]).wait()
+
     loads[2].wait()
-    for du in (4, 3, 5, 2, 6, 1, 7):
-        pltpu.make_async_remote_copy(new_all.at[u], new_all.at[u], new_send, new_recv,
-                                     device_id=at_row(plus(u, du), v), device_id_type=MESH).start()
+    for du in (2, 6, 1, 7):
+        hand(0, du)
 
     found = lax.dot_general(ranks[...].astype(BF16), row_hot[...], (((0,), (0,)), ((), ())), preferred_element_type=F32)
     own_y, own_z = own >> 3, own & (SIDE - 1)
-    own_uv = (own_y + (own_z - own_y) * core) * SIDE + own_z + (own_y - own_z) * core
+    own_u = own_y + (own_z - own_y) * core
+    own_v = own_z + (own_y - own_z) * core
+    nth = (3 * (u - own_u)) & (SIDE - 1)
+    batch = (3 * (v - own_v - nth)) & (SIDE - 1)
     for k in range(slots_row):
         cols = slice(k * new_dev, (k + 1) * new_dev)
         pos = jnp.sum(jnp.where(sub_lo == lo[k:k + 1, :], found[:, cols], 0.0), axis=0, keepdims=True)
-        code_own[k:k + 1, :] = jnp.where(live[k:k + 1, :], own_uv[k:k + 1, :] * DISTINCT + pos.astype(I32), -1)
+        pos = jnp.where(live[k:k + 1, :], pos.astype(I32), -n_row * DISTINCT)
+        code_own[k:k + 1, :] = (own_u * SIDE + own_v)[k:k + 1, :] * DISTINCT + pos
+        slot_wide[k] = jnp.broadcast_to((batch * SIDE + nth)[k:k + 1, :] * DISTINCT + pos, (8, new_dev))
     pltpu.make_async_copy(code_own, codes.at[u], code_recv).start()
     for du in (4, 3, 5, 2, 6, 1, 7):
         pltpu.make_async_remote_copy(code_own, codes.at[u], code_send, code_recv,
@@ -157,26 +169,33 @@
         else:
             pltpu.make_async_remote_copy(send_aux.at[dv], got_aux.at[v], aux_send, aux_recv,
                                          device_id=at_row(u, plus(v, dv)), device_id_type=MESH).start()
+    block_in(2)
+    hand(2, 2)
+    hand(2, 1)
+    block_in(6)
+    hand(6, 7)
     for dv in HOPS:
         gather(dv, emb_tab, send_emb)
 
-    def send_line(dv):
-        for du in (4, 3, 5, 2, 6, 1, 7, 0):
+    def send_line(q):
+        for p in range(SIDE):
+            du, dv = (3 * p) % SIDE, (3 * q + p) % SIDE
             uu, vv = plus(u, du), plus(v, dv)
             if (du, dv) == (0, 0):
-                pltpu.make_async_copy(send_emb.at[0, u], got_emb.at[u * SIDE + v], emb_recv).start()
+                pltpu.make_async_copy(send_emb.at[0, u], got_emb.at[0], emb_recv.at[0]).start()
             else:
-                pltpu.make_async_remote_copy(send_emb.at[dv, uu], got_emb.at[u * SIDE + v], emb_send, emb_recv,
+                pltpu.make_async_remote_copy(send_emb.at[dv, uu], got_emb.at[q * SIDE + p], emb_send, emb_recv.at[q],
                                              device_id=at_row(uu, vv), device_id_type=MESH).start()
 
     total_of(send_aux.at[pl.ds(0, SIDE - 1)], aux_send).wait()
-    for dv in HOPS[:EARLY]:
-        send_line(dv)
+    for q in range(EARLY):
+        send_line(q)
 
     own_sq = jnp.sum(jnp.square(new_all[u].astype(F32)), axis=1, keepdims=True)
     part[2 * slots_row:2 * slots_row + 8, :] = jnp.broadcast_to(own_sq, (new_dev, LANES)).T[0:8, :]
 
-    total_of(new_all.at[pl.ds(0, SIDE - 1)], new_recv).wait()
+    for block in (1, 7, 3, 5, 4):
+        block_in(block)
     total_of(codes, code_recv).wait()
     total_of(got_aux, aux_recv).wait()
 
@@ -207,11 +226,9 @@
         else:
             pltpu.make_async_remote_copy(met.at[uu], gath.at[u], met_send, met_recv,
                                          device_id=at_row(uu, v), device_id_type=MESH).start()
-    for dv in HOPS[EARLY:]:
-        send_line(dv)
-
-    for k in range(slots_row):
-        slot_wide[k] = jnp.broadcast_to(code_own[k:k + 1, :], (8, new_dev))
+    for q in range(EARLY, SIDE):
+        send_line(q)
+
     total_of(gath, met_recv).wait()
     both = gath[0]
     for a in range(1, SIDE):
@@ -245,9 +262,13 @@
     lax.fori_loop(0, n_row, weigh, 0)
     w_t = w_slots[...].T.astype(BF16)
 
-    total_of(got_emb, emb_recv).wait()
-    near_emb = got_emb[...].reshape(n_row * DISTINCT, width)
-    out_ref[...] = jnp.dot(w_t, near_emb, preferred_element_type=F32).astype(BF16)
+    def blend(first, last):
+        for q in range(first, last):
+            total_of(got_emb.at[pl.ds(q * SIDE, SIDE)], emb_recv.at[q]).wait()
+        rows = got_emb[first * SIDE:last * SIDE].reshape((last - first) * line, width)
+        return jnp.dot(w_t[:, first * line:last * line], rows, preferred_element_type=F32)
+
+    out_ref[...] = (blend(0, SIDE - 2) + blend(SIDE - 2, SIDE)).astype(BF16)
 
     total_of(lists.at[pl.ds(0, n_row - 1)], list_send).wait()
     total_of(new_all.at[pl.ds(0, SIDE - 1)], new_send).wait()
@@ -287,8 +308,8 @@
                 vm((slots, new_dev), F32),
                 vm((SIDE, 2 * slots_row, new_dev), F32), vm((SIDE, 2 * slots_row, new_dev), F32),
                 vm((2 * slots_row + 8, new_dev), F32), vm((n_col - 1, 2 * slots_row + 8, new_dev), F32),
-                dma((5,)), dma(()), dma((SIDE,)), dma(()), dma(()), dma(()), dma(()), dma(()), dma(()),
-                dma(()), dma(()), dma(()), dma(()), dma(()), dma(()),
+                dma((5,)), dma(()), dma((SIDE,)), dma(()), dma((SIDE,)), dma(()), dma(()), dma(()), dma(()),
+                dma(()), dma((SIDE,)), dma(()), dma(()), dma(()), dma(()),
             ],
             compiler_params=pltpu.CompilerParams(
                 collective_id=0, has_side_effects=True, vmem_limit_bytes=67043328),

time: 100 us -> 88.3 us (0.88)
  Pallas kernels: 98.3 us -> 86.1 us
    pallas_call x1, Pallas kernels: 98.3 us -> 86.1 us  [local(): pl.pallas_call(functools.partial(kernel, n_row, n_col), out_shape=jax.Sha...]
where the time goes in v3:
time: 88.3 us; the launch traced here: 87.6 us
  Pallas kernels  86.1 us (98%)
  local copies, waits for them, and re-layouts  1.57 us (2%)
    pallas_call x1, Pallas kernels, local(): pl.pallas_call(functools.partial(kernel, n_row, n_col), out_shape=jax.Sha...  86.1 us

profile of v3, /device:TPU:1, one launch (start us, length us, event | category | flops | bytes accessed | tf_op | source)
XLA Modules:
  0.0 87.6 jit_solution(1706343704097896733)
XLA Ops:
  0.0 86.1 %shard_map.55 = bf16[128,512]{1,0:T(8,128)(2,1)} custom-call(s32[16,128]{1,0:T(8,128)} %bitcast.2, s32[1,128]{1,0:T(1,128)} %bitcast.3, bf16[128,512]{1,0:T(8,128)(2,1)} %new_hbm.1, bf16[1280,512]{1,0:T(8,128)(2,1)} %aux_hbm.1, bf16[1280,512]{1,0:T(8,128)(2,1)} %emb_hbm.1), custom_call_target="tpu_custom_call" | custom-call | tf_op jit(solution)/shard_map/pallas_call | solution.py:293
  86.1 1.6 %copy.7 = bf16[128,512]{1,0:T(8,128)(2,1)} copy(bf16[128,512]{1,0:T(8,128)(2,1)} %shard_map.55) | data formatting | bytes 262144

commit v4 on v3

--- a/solution.py
+++ b/solution.py
@@ -14,6 +14,7 @@
 LANES = 128
 HOPS = (4, 3, 5, 2, 6, 1, 7, 0)
 EARLY = 2
+LATE = 5
 eps = 1e-06
 exponential_sharpness = 0.025
 
@@ -126,15 +127,20 @@
         total_of(new_all.at[plus(u, -block)], new_recv.at[block]).wait()
 
     loads[2].wait()
-    for du in (2, 6, 1, 7):
-        hand(0, du)
+    hand(0, 1)
+    hand(0, 7)
 
     found = lax.dot_general(ranks[...].astype(BF16), row_hot[...], (((0,), (0,)), ((), ())), preferred_element_type=F32)
     own_y, own_z = own >> 3, own & (SIDE - 1)
     own_u = own_y + (own_z - own_y) * core
     own_v = own_z + (own_y - own_z) * core
-    nth = (3 * (u - own_u)) & (SIDE - 1)
-    batch = (3 * (v - own_v - nth)) & (SIDE - 1)
+
+    def place_of(d):
+        far = (d & (SIDE - 1)) - SIDE // 2
+        return jnp.where(far > 0, 2 * far, jnp.where(far < 0, -2 * far - 1, 0))
+
+    nth = place_of(u - own_u)
+    batch = place_of(v - own_v - 3 * (u - own_u))
     for k in range(slots_row):
         cols = slice(k * new_dev, (k + 1) * new_dev)
         pos = jnp.sum(jnp.where(sub_lo == lo[k:k + 1, :], found[:, cols], 0.0), axis=0, keepdims=True)
@@ -145,6 +151,11 @@
     for du in (4, 3, 5, 2, 6, 1, 7):
         pltpu.make_async_remote_copy(code_own, codes.at[u], code_send, code_recv,
                                      device_id=at_row(plus(u, du), v), device_id_type=MESH).start()
+
+    block_in(1)
+    hand(1, 1)
+    block_in(7)
+    hand(7, 7)
 
     loads[3].wait()
     loads[4].wait()
@@ -170,34 +181,35 @@
             pltpu.make_async_remote_copy(send_aux.at[dv], got_aux.at[v], aux_send, aux_recv,
                                          device_id=at_row(u, plus(v, dv)), device_id_type=MESH).start()
     block_in(2)
-    hand(2, 2)
     hand(2, 1)
     block_in(6)
     hand(6, 7)
     for dv in HOPS:
         gather(dv, emb_tab, send_emb)
+    block_in(3)
+    hand(3, 1)
 
     def send_line(q):
         for p in range(SIDE):
-            du, dv = (3 * p) % SIDE, (3 * q + p) % SIDE
+            du = HOPS[p]
+            dv = (3 * du + HOPS[q]) % SIDE
             uu, vv = plus(u, du), plus(v, dv)
             if (du, dv) == (0, 0):
-                pltpu.make_async_copy(send_emb.at[0, u], got_emb.at[0], emb_recv.at[0]).start()
+                pltpu.make_async_copy(send_emb.at[0, u], got_emb.at[q * SIDE + p], emb_recv.at[q]).start()
             else:
                 pltpu.make_async_remote_copy(send_emb.at[dv, uu], got_emb.at[q * SIDE + p], emb_send, emb_recv.at[q],
                                              device_id=at_row(uu, vv), device_id_type=MESH).start()
 
-    total_of(send_aux.at[pl.ds(0, SIDE - 1)], aux_send).wait()
+
+    own_sq = jnp.sum(jnp.square(new_all[u].astype(F32)), axis=1, keepdims=True)
+    part[2 * slots_row:2 * slots_row + 8, :] = jnp.broadcast_to(own_sq, (new_dev, LANES)).T[0:8, :]
+
+    block_in(5)
+    block_in(4)
+    total_of(codes, code_recv).wait()
+    total_of(got_aux, aux_recv).wait()
     for q in range(EARLY):
         send_line(q)
-
-    own_sq = jnp.sum(jnp.square(new_all[u].astype(F32)), axis=1, keepdims=True)
-    part[2 * slots_row:2 * slots_row + 8, :] = jnp.broadcast_to(own_sq, (new_dev, LANES)).T[0:8, :]
-
-    for block in (1, 7, 3, 5, 4):
-        block_in(block)
-    total_of(codes, code_recv).wait()
-    total_of(got_aux, aux_recv).wait()
 
     sub8 = iota((8, new_dev), 0)
 
@@ -226,10 +238,12 @@
         else:
             pltpu.make_async_remote_copy(met.at[uu], gath.at[u], met_send, met_recv,
                                          device_id=at_row(uu, v), device_id_type=MESH).start()
-    for q in range(EARLY, SIDE):
+    for q in range(EARLY, LATE):
         send_line(q)
 
     total_of(gath, met_recv).wait()
+    for q in range(LATE, SIDE):
+        send_line(q)
     both = gath[0]
     for a in range(1, SIDE):
         both = both + gath[a]
@@ -271,6 +285,7 @@
     out_ref[...] = (blend(0, SIDE - 2) + blend(SIDE - 2, SIDE)).astype(BF16)
 
     total_of(lists.at[pl.ds(0, n_row - 1)], list_send).wait()
+    total_of(send_aux.at[pl.ds(0, SIDE - 1)], aux_send).wait()
     total_of(new_all.at[pl.ds(0, SIDE - 1)], new_send).wait()
     total_of(codes.at[pl.ds(0, SIDE - 1)], code_send).wait()
     total_of(got_emb.at[pl.ds(0, n_row - 1)], emb_send).wait()

time: 88.3 us -> 86.7 us (0.982)
  Pallas kernels: 86.1 us -> 84.9 us
    pallas_call x1, Pallas kernels: 86.1 us -> 84.9 us  [local(): pl.pallas_call(functools.partial(kernel, n_row, n_col), out_shape=jax.Sha...]
where the time goes in v4:
time: 86.7 us; the launch traced here: 86.5 us
  Pallas kernels  84.9 us (98%)
  local copies, waits for them, and re-layouts  1.57 us (2%)
    pallas_call x1, Pallas kernels, local(): pl.pallas_call(functools.partial(kernel, n_row, n_col), out_shape=jax.Sha...  84.9 us

profile of v4, /device:TPU:1, one launch (start us, length us, event | category | flops | bytes accessed | tf_op | source)
XLA Modules:
  0.0 86.5 jit_solution(13166517423373888614)
XLA Ops:
  0.0 84.9 %shard_map.55 = bf16[128,512]{1,0:T(8,128)(2,1)} custom-call(s32[16,128]{1,0:T(8,128)} %bitcast.2, s32[1,128]{1,0:T(1,128)} %bitcast.3, bf16[128,512]{1,0:T(8,128)(2,1)} %new_hbm.1, bf16[1280,512]{1,0:T(8,128)(2,1)} %aux_hbm.1, bf16[1280,512]{1,0:T(8,128)(2,1)} %emb_hbm.1), custom_call_target="tpu_custom_call" | custom-call | tf_op jit(solution)/shard_map/pallas_call | solution.py:308
  84.9 1.6 %copy.7 = bf16[128,512]{1,0:T(8,128)(2,1)} copy(bf16[128,512]{1,0:T(8,128)(2,1)} %shard_map.55) | data formatting | bytes 262144

commit v5 on v4

--- a/solution.py
+++ b/solution.py
@@ -184,10 +184,12 @@
     hand(2, 1)
     block_in(6)
     hand(6, 7)
-    for dv in HOPS:
+    for dv in HOPS[:4]:
         gather(dv, emb_tab, send_emb)
     block_in(3)
     hand(3, 1)
+    for dv in HOPS[4:]:
+        gather(dv, emb_tab, send_emb)
 
     def send_line(q):
         for p in range(SIDE):

time: 86.7 us -> 86.7 us (level)
  no operation moved by 1% of the time
where the time goes in v5:
time: 86.7 us; the launch traced here: 86.5 us
  Pallas kernels  84.9 us (98%)
  local copies, waits for them, and re-layouts  1.57 us (2%)
    pallas_call x1, Pallas kernels, local(): pl.pallas_call(functools.partial(kernel, n_row, n_col), out_shape=jax.Sha...  84.9 us

profile of v5, /device:TPU:1, one launch (start us, length us, event | category | flops | bytes accessed | tf_op | source)
XLA Modules:
  0.0 86.5 jit_solution(10508776462962613802)
XLA Ops:
  0.0 84.9 %shard_map.55 = bf16[128,512]{1,0:T(8,128)(2,1)} custom-call(s32[16,128]{1,0:T(8,128)} %bitcast.2, s32[1,128]{1,0:T(1,128)} %bitcast.3, bf16[128,512]{1,0:T(8,128)(2,1)} %new_hbm.1, bf16[1280,512]{1,0:T(8,128)(2,1)} %aux_hbm.1, bf16[1280,512]{1,0:T(8,128)(2,1)} %emb_hbm.1), custom_call_target="tpu_custom_call" | custom-call | tf_op jit(solution)/shard_map/pallas_call | solution.py:310
  84.9 1.6 %copy.7 = bf16[128,512]{1,0:T(8,128)(2,1)} copy(bf16[128,512]{1,0:T(8,128)(2,1)} %shard_map.55) | data formatting | bytes 262144
